TPU v7x, 32 devices: a whole 2x2x4 slice. The times are simulated.
32 devices in a mesh: replica: 4 (over x, core), fsdp: 8 (over z, y).
Axes of the slice: x: 2, y: 2, z: 4, core: 2. Of those that a mesh axis runs over, the one named last changes fastest.
Arguments:
- deltas: bfloat16 [4, 2, 2048, 16384], P('replica', None, 'fsdp'), may hold values from -3 to 3
- master: float32 [2, 2048, 16384], P(None, 'replica', 'fsdp'), may hold values from -3 to 3
- momentum: float32 [2, 2048, 16384], P(None, 'replica', 'fsdp'), may hold values from -2 to 2
Outputs:
- master_out: float32 [2, 2048, 16384], P(None, 'replica', 'fsdp')
- momentum_out: float32 [2, 2048, 16384], P(None, 'replica', 'fsdp')
- params_out: bfloat16 [2, 2048, 16384], P(None, 'fsdp')
All inputs are finite; a program needn't handle non-finite values.
Results may differ from a plain program's by a relative error of at most 0.008.
Values may be sent and summed in bfloat16 or wider, within the bound.
A program may use at most 128 MiB of HBM per device.

v0:
```python
import functools

import jax
import jax.numpy as jnp
from jax import lax
from jax.experimental import pallas as pl
from jax.experimental.pallas import tpu as pltpu
from jax.sharding import PartitionSpec as P

F32, BF16 = jnp.float32, jnp.bfloat16
SPLITS = 4
AHEAD = 4
LAGS = (2, 5, 8, 10)


def kernel(
    dims, delta, master, momentum, master_out, momentum_out, out,
    own, half, cross, total, mas, mom,
    load, store, sent, pair_a, pair_b, cross_in, cross_side, total_in, back_in, side_in, last_in,
):
    R, F, PROJ, RB, FF, WD, H = dims
    B, X = F // R, R // PROJ
    RH, SUB, T = RB // X, WD // H, F * H
    w, f = lax.axis_index("replica"), lax.axis_index("fsdp")
    core, x = lax.rem(w, PROJ), w // PROJ
    a, b = f // B, lax.rem(f, B)
    other = 1 - core
    w_pair = x * PROJ + other
    w_side = (1 - x) * PROJ + core
    w_far = (1 - x) * PROJ + other
    pair, side = (w_pair, f), (w_side, f)
    near = x == a // PROJ
    far = jnp.logical_not(near)

    def turned(t):
        return lax.rem(t + t // F, 2) == 1

    def to(ref_src, ref_dst, send, recv, device):
        return pltpu.make_async_remote_copy(
            src_ref=ref_src, dst_ref=ref_dst, send_sem=send, recv_sem=recv,
            device_id=device, device_id_type=pl.DeviceIdType.MESH,
        )

    def block(worker, t):
        return lax.rem(lax.rem(t, F) + f + worker * B, F)

    def cols(worker, t):
        return pl.ds(pl.multiple_of(block(worker, t) * WD + (t // F) * SUB, 128), SUB)

    def rows(xi):
        return pl.ds(pl.multiple_of(xi * RH, RH), RH)

    def drain(ref, sem):
        pltpu.make_async_copy(ref, ref, sem).wait()

    barrier = pltpu.get_barrier_semaphore()
    mine = a == w

    def greet(device):
        pl.semaphore_signal(barrier, inc=1, device_id=device, device_id_type=pl.DeviceIdType.MESH)

    load_own = pltpu.make_async_copy(delta.at[core], own, load.at[0])
    load_mas = pltpu.make_async_copy(master, mas, load.at[1])
    load_mom = pltpu.make_async_copy(momentum, mom, load.at[2])
    load_own.start()
    load_mas.start()
    load_mom.start()
    greet(pair)
    greet(side)

    @pl.loop(0, F)
    def _(i):
        @pl.when(jnp.logical_not(jnp.logical_and(mine, i == f)))
        def _():
            greet((a, i))

        wi, bi = i // B, lax.rem(i, B)

        @pl.when(jnp.logical_not(jnp.logical_and(mine, jnp.logical_and(wi == w, bi == b))))
        def _():
            greet((wi, w * B + bi))

    @pl.when(mine)
    def _():
        pl.semaphore_wait(barrier, 2 * F)

    @pl.when(jnp.logical_not(mine))
    def _():
        pl.semaphore_wait(barrier, 2 * F + 2)

    def send_pair(t):
        cb, ca = cols(w_far, t), cols(w_pair, t)
        src = delta.at[other]
        to(src.at[rows(1 - x), cb], half.at[rows(1 - x), cb], sent.at[0], pair_b.at[t], pair).start()
        to(src.at[rows(x), ca], half.at[rows(x), ca], sent.at[0], pair_a.at[t], pair).start()

    def pair_sum(xi, c, arrived, send, recv):
        tile, mine_tile = half.at[rows(xi), c], own.at[rows(xi), c]
        pltpu.make_async_copy(tile, tile, arrived).wait()
        tile[...] = (tile[...].astype(F32) + mine_tile[...].astype(F32)).astype(BF16)
        to(tile, cross.at[rows(xi), c], send, recv, side).start()

    def step_cross(t):
        turn = turned(t)

        @pl.when(jnp.logical_not(jnp.logical_and(near, turn)))
        def _():
            pair_sum(1 - x, cols(w_side, t), pair_b.at[t], sent.at[1], cross_in.at[t])

        @pl.when(jnp.logical_and(far, turn))
        def _():
            pair_sum(x, cols(w, t), pair_a.at[t], sent.at[7], cross_side.at[t])

    def owner_slot(pi, bi, xi, t):
        return total.at[
            pi,
            pl.ds(pl.multiple_of(bi * RB + xi * RH, RH), RH),
            pl.ds(pl.multiple_of((t // F) * SUB, 128), SUB),
        ]

    def full_sum(worker, xi, t, arrived_pair, arrived_cross, send):
        c = cols(worker, t)
        tile, mine_tile, arrived = half.at[rows(xi), c], own.at[rows(xi), c], cross.at[rows(xi), c]
        pltpu.make_async_copy(tile, tile, arrived_pair).wait()
        pltpu.make_async_copy(arrived, arrived, arrived_cross).wait()
        tile[...] = (
            tile[...].astype(F32) + mine_tile[...].astype(F32) + arrived[...].astype(F32)
        ).astype(BF16)
        cb = block(worker, t)
        slot = owner_slot(core, b, xi, t)
        here = jnp.logical_and(mine, cb == f)

        @pl.when(here)
        def _():
            pltpu.make_async_copy(tile, slot, total_in.at[t]).start()

        @pl.when(jnp.logical_not(here))
        def _():
            to(tile, slot, send, total_in.at[t], (a, cb)).start()

    def step_total(t):
        turn = turned(t)

        @pl.when(jnp.logical_or(near, jnp.logical_not(turn)))
        def _():
            full_sum(w, x, t, pair_a.at[t], cross_in.at[t], sent.at[2])

        @pl.when(jnp.logical_and(near, turn))
        def _():
            full_sum(w_side, 1 - x, t, pair_b.at[t], cross_side.at[t], sent.at[6])

    def step_update(t):
        e = lax.rem(f + 2 * F - lax.rem(t, F) - w * B, F)
        we, be = e // B, lax.rem(e, B)
        pe, xe = lax.rem(we, PROJ), we // PROJ
        r0 = pl.multiple_of(be * RB + xe * RH, RH)
        rr = pl.ds(r0, RH)
        cc = pl.ds(pl.multiple_of((t // F) * SUB, 128), SUB)
        tile = owner_slot(pe, be, xe, t)
        pltpu.make_async_copy(tile, tile, total_in.at[t]).wait()
        m, v = mas.at[pe, rr, cc], mom.at[pe, rr, cc]
        outer = tile[...].astype(F32) / R
        velocity = 0.9 * v[...] + outer
        updated = m[...] - 0.7 * (outer + 0.9 * velocity)
        v[...] = velocity
        m[...] = updated
        tile[...] = updated.astype(BF16)
        pltpu.make_async_copy(m, master_out.at[pe, rr, cc], store.at[0]).start()
        pltpu.make_async_copy(v, momentum_out.at[pe, rr, cc], store.at[1]).start()
        fe = w * B + be
        dst = out.at[pe, rows(xe), pl.ds(pl.multiple_of(f * WD + (t // F) * SUB, 128), SUB)]
        here = jnp.logical_and(we == w, fe == f)

        @pl.when(here)
        def _():
            pltpu.make_async_copy(tile, dst, back_in.at[t]).start()

        @pl.when(jnp.logical_not(here))
        def _():
            to(tile, dst, sent.at[3], back_in.at[t], (we, fe)).start()

    def step_side(t):
        tile = out.at[core, rows(x), cols(w, t)]
        pltpu.make_async_copy(tile, tile, back_in.at[t]).wait()
        to(tile, tile, sent.at[4], side_in.at[t], side).start()
        to(tile, tile, sent.at[5], last_in, pair).start()

    def step_pair(t):
        tile = out.at[core, rows(1 - x), cols(w_side, t)]
        pltpu.make_async_copy(tile, tile, side_in.at[t]).wait()
        to(tile, tile, sent.at[5], last_in, pair).start()

    @pl.loop(0, min(AHEAD, T))
    def _(t):
        send_pair(t)

    load_own.wait()

    @pl.loop(0, T + LAGS[-1])
    def _(t):
        @pl.when(t + AHEAD < T)
        def _():
            send_pair(t + AHEAD)

        @pl.when(t < T)
        def _():
            step_cross(t)

        @pl.when(t == LAGS[1])
        def _():
            load_mas.wait()
            load_mom.wait()

        for lag, step in zip(LAGS, (step_total, step_update, step_side, step_pair)):
            @pl.when(jnp.logical_and(t >= lag, t < T + lag))
            def _():
                step(t - lag)

    drain(out.at[other], last_in)
    drain(half, sent.at[0])

    def drain_part(width, sem):
        drain(half.at[pl.ds(0, RH), pl.ds(0, width)], sem)

    @pl.when(mine)
    def _():
        drain_part(FF - WD, sent.at[2])
        drain_part((FF - WD) // 2, sent.at[6])
        drain_part(FF - WD, sent.at[3])

    @pl.when(jnp.logical_not(mine))
    def _():
        drain_part(FF, sent.at[3])

    @pl.when(jnp.logical_and(near, jnp.logical_not(mine)))
    def _():
        drain_part(FF, sent.at[2])
        drain_part(FF // 2, sent.at[6])

    @pl.when(near)
    def _():
        drain_part(FF // 2, sent.at[1])

    @pl.when(far)
    def _():
        drain_part(FF, sent.at[1])
        drain_part(FF // 2, sent.at[2])
        drain_part(FF // 2, sent.at[7])

    drain_part(FF, sent.at[4])
    drain(half, sent.at[5])
    drain(mas, store.at[0])
    drain(mom, store.at[1])


def on_device(deltas, master, momentum):
    local = deltas[0]
    R, F = lax.axis_size("replica"), lax.axis_size("fsdp")
    PROJ, RB, FF = local.shape
    WD = FF // F
    H = min(SPLITS, WD // 128)
    assert R == 2 * PROJ and PROJ == 2 and F % R == 0 and H % 2 == 0
    T = F * H
    hbm = pl.BlockSpec(memory_space=pl.ANY)
    dma = pltpu.SemaphoreType.DMA
    updated, velocity, params = pl.pallas_call(
        functools.partial(kernel, (R, F, PROJ, RB, FF, WD, H)),
        out_shape=(
            jax.ShapeDtypeStruct(master.shape, F32),
            jax.ShapeDtypeStruct(momentum.shape, F32),
            jax.ShapeDtypeStruct(local.shape, BF16),
        ),
        in_specs=[hbm] * 3,
        out_specs=(hbm,) * 3,
        scratch_shapes=[
            pltpu.VMEM((RB, FF), BF16),
            pltpu.VMEM((RB, FF), BF16),
            pltpu.VMEM((RB, FF), BF16),
            pltpu.VMEM(master.shape, BF16),
            pltpu.VMEM(master.shape, F32),
            pltpu.VMEM(master.shape, F32),
            dma((3,)), dma((2,)), dma((8,)),
            dma((T,)), dma((T,)), dma((T,)), dma((T,)), dma((T,)), dma((T,)), dma((T,)), dma,
        ],
        compiler_params=pltpu.CompilerParams(
            collective_id=0, has_side_effects=True, vmem_limit_bytes=56 * 2**20
        ),
    )(local, master, momentum)
    return updated, velocity, params


def solution(mesh):
    return jax.shard_map(
        on_device,
        mesh=mesh,
        in_specs=(
            P("replica", None, "fsdp", None),
            P(None, "replica", "fsdp"),
            P(None, "replica", "fsdp"),
        ),
        out_specs=(P(None, "replica", "fsdp"), P(None, "replica", "fsdp"), P(None, "fsdp", None)),
        check_vma=False,
    )
```

profile of v0, /device:TPU:3, one launch (start us, length us, event | category | flops | bytes accessed | tf_op | source)
XLA Modules:
  0.0 292.1 jit_solution(10104386146694173061)
XLA Ops:
  0.6 268.3 %shard_map.58 = (f32[2,512,2048]{2,1,0:T(8,128)}, f32[2,512,2048]{2,1,0:T(8,128)}, bf16[2,256,16384]{2,1,0:T(8,128)(2,1)}) custom-call(bf16[2,256,16384]{2,1,0:T(8,128)(2,1)} %bitcast.1, f32[2,512,2048]{2,1,0:T(8,128)} %master.1, f32[2,512,2048]{2,1,0:T(8,128)} %momentum.1), custom_call_target="tpu_custom_call" | custom-call | tf_op jit(solution)/shard_map/pallas_call | solution.py:266
  268.9 0.0 slice-start
  269.0 0.0 slice-start.1
  269.0 0.0 slice-start.2
  269.0 8.9 %copy.9 = f32[2,512,2048]{2,1,0:T(8,128)} copy(f32[2,512,2048]{2,1,0:T(8,128)} %get-tuple-element.6) | data formatting | bytes 16777216
  277.9 0.0 slice-start.3
  277.9 8.0 %copy.10 = f32[2,512,2048]{2,1,0:T(8,128)} copy(f32[2,512,2048]{2,1,0:T(8,128)} %get-tuple-element.7) | data formatting | bytes 16777216
  285.9 0.0 slice-done
  285.9 0.0 slice-done.1
  285.9 0.0 slice-done.2
  285.9 0.0 slice-done.3
  285.9 6.2 %copy.11 = bf16[2,256,16384]{2,1,0:T(8,128)(2,1)} copy(bf16[2,256,16384]{2,1,0:T(8,128)(2,1)S(1)} %bitcast.3) | data formatting | bytes 33554432
  (1 shorter events, 0.0 us)
Async XLA Ops:
  268.9 17.0 %slice-start = ((s8[16777216]{0:T(1024)(128)(4,1)}), s8[4194304]{0:T(1024)(128)(4,1)S(1)}, s32[]{:S(2)}) async-start(s8[16777216]{0:T(1024)(128)(4,1)} %bitcast.2), calls=%async_computation | async-start | bytes 8388608
  269.0 17.0 %slice-start.1 = ((s8[16777216]{0:T(1024)(128)(4,1)}), s8[4194304]{0:T(1024)(128)(4,1)S(1)}, s32[]{:S(2)}) async-start(s8[16777216]{0:T(1024)(128)(4,1)} %bitcast.2), calls=%async_computation.1 | async-start | bytes 8388608
  269.0 17.0 %slice-start.2 = ((s8[16777216]{0:T(1024)(128)(4,1)}), s8[4194304]{0:T(1024)(128)(4,1)S(1)}, s32[]{:S(2)}) async-start(s8[16777216]{0:T(1024)(128)(4,1)} %bitcast.2), calls=%async_computation.2 | async-start | bytes 8388608
  277.9 8.1 %slice-start.3 = ((s8[16777216]{0:T(1024)(128)(4,1)}), s8[4194304]{0:T(1024)(128)(4,1)S(1)}, s32[]{:S(2)}) async-start(s8[16777216]{0:T(1024)(128)(4,1)} %bitcast.2), calls=%async_computation.3 | async-start | bytes 8388608
where the time goes:
time: 294 us; the launch traced here: 292 us
  Pallas kernels  268 us (91%)
  local copies, waits for them, and re-layouts  23.1 us (8%)
    pallas_call x1, Pallas kernels, on_device(): pl.pallas_call(functools.partial(kernel, (R, F, PROJ, RB, FF, WD, H)), ou...  268 us
    unnamed x11, local copies, waits for them, and re-layouts  23.1 us

commit v1 on v0

v1 whole, which is shorter than its diff:
```python
import functools

import jax
import jax.numpy as jnp
from jax import lax
from jax.experimental import pallas as pl
from jax.experimental.pallas import tpu as pltpu
from jax.sharding import PartitionSpec as P

F32, BF16 = jnp.float32, jnp.bfloat16
SPLITS = 16
AHEAD = 8
LAGS = (4, 8, 12, 15)


def kernel(
    dims, delta, master, momentum, mas, mom, out,
    half, cross, total,
    load, load_own, sent, pair_in, cross_in, total_in, back_in, side_in, last_in,
):
    R, F, PROJ, RB, FF, WD, H = dims
    B, S, T = F // R, RB // H, F * H
    w, f = lax.axis_index("replica"), lax.axis_index("fsdp")
    core, x = lax.rem(w, PROJ), w // PROJ
    a, b = f // B, lax.rem(f, B)
    other = 1 - core
    pair = (x * PROJ + other, f)
    side = ((1 - x) * PROJ + core, f)
    near = x == a // PROJ
    far = jnp.logical_not(near)
    mine = a == w

    def to(ref_src, ref_dst, send, recv, device):
        return pltpu.make_async_remote_copy(
            src_ref=ref_src, dst_ref=ref_dst, send_sem=send, recv_sem=recv,
            device_id=device, device_id_type=pl.DeviceIdType.MESH,
        )

    def drain(ref, sem):
        pltpu.make_async_copy(ref, ref, sem).wait()

    def block(c, t):
        return lax.rem(lax.rem(t, F) + f + c * (F // 2), F)

    def rows(t):
        return pl.ds(pl.multiple_of((t // F) * S, S), S)

    def cols(i):
        return pl.ds(pl.multiple_of(i * WD, 128), WD)

    def own_rows(h):
        r = pl.ds(pl.multiple_of(h * S, S), S)
        return pltpu.make_async_copy(delta.at[core, r], out.at[core, r], load_own.at[h])

    barrier = pltpu.get_barrier_semaphore()

    def greet(device):
        pl.semaphore_signal(barrier, inc=1, device_id=device, device_id_type=pl.DeviceIdType.MESH)

    greet(pair)
    greet(side)

    @pl.loop(0, PROJ * B)
    def _(i):
        p, bi = i // B, lax.rem(i, B)

        @pl.when(jnp.logical_not(jnp.logical_and(mine, jnp.logical_and(p == core, bi == b))))
        def _():
            greet((x * PROJ + p, w * B + bi))

    @pl.when(near)
    def _():
        @pl.loop(0, F)
        def _(i):
            @pl.when(jnp.logical_not(jnp.logical_and(mine, i == f)))
            def _():
                greet((a, i))

    @pl.loop(0, H)
    def _(h):
        own_rows(h).start()

    @pl.when(far)
    def _():
        pl.semaphore_wait(barrier, 2 + PROJ * B)

    @pl.when(mine)
    def _():
        pl.semaphore_wait(barrier, PROJ * B + F)

    @pl.when(jnp.logical_and(near, jnp.logical_not(mine)))
    def _():
        pl.semaphore_wait(barrier, 2 + PROJ * B + F)

    def send_pair(t):
        c = cols(block(other, t))
        to(delta.at[other, rows(t), c], half.at[rows(t), c], sent.at[0], pair_in.at[t], pair).start()

    def step_cross(t):
        @pl.when(lax.rem(t, F) == 0)
        def _():
            own_rows(t // F).wait()

        r, c = rows(t), cols(block(core, t))
        tile = half.at[r, c]
        pltpu.make_async_copy(tile, tile, pair_in.at[t]).wait()
        tile[...] = (tile[...].astype(F32) + out[core, r, c].astype(F32)).astype(BF16)
        to(tile, cross.at[r, c], sent.at[1], cross_in.at[t], side).start()

    def slot(p, bi, h):
        return total.at[p, pl.ds(pl.multiple_of(bi * RB + h * S, S), S)]

    def step_total(t):
        h = t // F

        @pl.when(lax.rem(t, F) == 0)
        def _():
            own_rows(h).wait()

        i = block(core, t)
        r, c = rows(t), cols(i)
        tile, arrived = half.at[r, c], cross.at[r, c]
        pltpu.make_async_copy(tile, tile, pair_in.at[t]).wait()
        pltpu.make_async_copy(arrived, arrived, cross_in.at[t]).wait()
        tile[...] = (
            tile[...].astype(F32) + out[core, r, c].astype(F32) + arrived[...].astype(F32)
        ).astype(BF16)
        dst, sem = slot(core, b, h), total_in.at[(core * B + b) * H + h]
        here = jnp.logical_and(mine, i == f)

        @pl.when(here)
        def _():
            pltpu.make_async_copy(tile, dst, sem).start()

        @pl.when(jnp.logical_not(here))
        def _():
            to(tile, dst, sent.at[2], sem, (a, i)).start()

    def step_update(t):
        h, k = t // F, lax.rem(t, F)
        for p in range(PROJ):
            e = lax.rem(f + 2 * F - k - p * (F // 2), F)

            @pl.when(e // B == w)
            def _():
                be = lax.rem(e, B)
                tile = slot(p, be, h)
                pltpu.make_async_copy(tile, tile, total_in.at[(p * B + be) * H + h]).wait()
                rr = pl.ds(pl.multiple_of(be * RB + h * S, S), S)
                outer = tile[...].astype(F32) / R
                velocity = 0.9 * mom[p, rr] + outer
                updated = mas[p, rr] - 0.7 * (outer + 0.9 * velocity)
                mom[p, rr] = velocity
                mas[p, rr] = updated
                tile[...] = updated.astype(BF16)
                dst = out.at[p, rows(t), cols(f)]
                here = jnp.logical_and(mine, jnp.logical_and(p == core, e == f))

                @pl.when(here)
                def _():
                    pltpu.make_async_copy(tile, dst, back_in.at[t]).start()

                @pl.when(jnp.logical_not(here))
                def _():
                    to(tile, dst, sent.at[3], back_in.at[t], (x * PROJ + p, e)).start()

    def step_side(t):
        tile = out.at[core, rows(t), cols(block(core, t))]
        pltpu.make_async_copy(tile, tile, back_in.at[t]).wait()
        to(tile, tile, sent.at[4], side_in.at[t], side).start()
        to(tile, tile, sent.at[5], last_in, pair).start()

    def step_pair(t):
        tile = out.at[core, rows(t), cols(block(core, t))]
        pltpu.make_async_copy(tile, tile, side_in.at[t]).wait()
        to(tile, tile, sent.at[5], last_in, pair).start()

    @pl.loop(0, min(AHEAD, T))
    def _(t):
        send_pair(t)

    load_mas = pltpu.make_async_copy(master, mas, load.at[0])
    load_mom = pltpu.make_async_copy(momentum, mom, load.at[1])

    @pl.loop(0, T + LAGS[-1])
    def _(t):
        @pl.when(t + AHEAD < T)
        def _():
            send_pair(t + AHEAD)

        @pl.when(jnp.logical_and(far, t < T))
        def _():
            step_cross(t)

        @pl.when(t == 0)
        def _():
            load_mas.start()
            load_mom.start()

        @pl.when(t == LAGS[1])
        def _():
            load_mas.wait()
            load_mom.wait()

        def late(lag, on, step):
            @pl.when(jnp.logical_and(on, jnp.logical_and(t >= lag, t < T + lag)))
            def _():
                step(t - lag)

        late(LAGS[0], near, step_total)
        late(LAGS[1], True, step_update)
        late(LAGS[2], near, step_side)
        late(LAGS[3], far, step_pair)

    drain(out.at[other], last_in)
    drain(half, sent.at[0])
    drain(half, sent.at[5])

    def drain_blocks(n, sem):
        drain(half.at[pl.ds(0, RB), pl.ds(0, n * WD)], sem)

    @pl.when(far)
    def _():
        drain_blocks(F, sent.at[1])
        drain_blocks(PROJ * B, sent.at[3])

    @pl.when(near)
    def _():
        drain_blocks(F, sent.at[4])

    @pl.when(mine)
    def _():
        drain_blocks(F - 1, sent.at[2])
        drain_blocks(PROJ * B - 1, sent.at[3])

    @pl.when(jnp.logical_and(near, jnp.logical_not(mine)))
    def _():
        drain_blocks(F, sent.at[2])
        drain_blocks(PROJ * B, sent.at[3])


def on_device(deltas, master, momentum):
    local = deltas[0]
    R, F = lax.axis_size("replica"), lax.axis_size("fsdp")
    PROJ, RB, FF = local.shape
    WD = FF // F
    H = min(SPLITS, RB // 16)
    assert R == 2 * PROJ and PROJ == 2 and F % R == 0 and RB % H == 0 and WD % 128 == 0
    T, B = F * H, F // R
    hbm, vmem = pl.BlockSpec(memory_space=pl.ANY), pl.BlockSpec(memory_space=pltpu.VMEM)
    dma = pltpu.SemaphoreType.DMA
    results = pl.pallas_call(
        functools.partial(kernel, (R, F, PROJ, RB, FF, WD, H)),
        out_shape=(
            pltpu.VMEM(master.shape, F32),
            pltpu.VMEM(momentum.shape, F32),
            pltpu.VMEM(local.shape, BF16),
        ),
        in_specs=[hbm] * 3,
        out_specs=(vmem,) * 3,
        scratch_shapes=[
            pltpu.VMEM((RB, FF), BF16),
            pltpu.VMEM((RB, FF), BF16),
            pltpu.VMEM(master.shape, BF16),
            dma((2,)), dma((H,)), dma((6,)),
            dma((T,)), dma((T,)), dma((PROJ * B * H,)), dma((T,)), dma((T,)), dma,
        ],
        compiler_params=pltpu.CompilerParams(
            collective_id=0, has_side_effects=True, vmem_limit_bytes=24 * 2**20
        ),
    )(local, master, momentum)
    return results


def solution(mesh):
    return jax.shard_map(
        on_device,
        mesh=mesh,
        in_specs=(
            P("replica", None, "fsdp", None),
            P(None, "replica", "fsdp"),
            P(None, "replica", "fsdp"),
        ),
        out_specs=(P(None, "replica", "fsdp"), P(None, "replica", "fsdp"), P(None, "fsdp", None)),
        check_vma=False,
    )
```

time: 294 us -> 226 us (0.77)
  Pallas kernels: 268 us -> 212 us
  local copies, waits for them, and re-layouts: 23.1 us -> 13 us
    pallas_call x1, Pallas kernels: 268 us -> 212 us  [on_device(): pl.pallas_call(functools.partial(kernel, (R, F, PROJ, RB, FF, WD, H)), ou...]
    unnamed x11 -> x3, local copies, waits for them, and re-layouts: 23.1 us -> 13 us
where the time goes in v1:
time: 226 us
  Pallas kernels  212 us (94%)
  local copies, waits for them, and re-layouts  13 us (6%)
    pallas_call x1, Pallas kernels, on_device(): pl.pallas_call(functools.partial(kernel, (R, F, PROJ, RB, FF, WD, H)), ou...  212 us
    unnamed x3, local copies, waits for them, and re-layouts  13 us

profile of v1, /device:TPU:3, one launch (start us, length us, event | category | flops | bytes accessed | tf_op | source)
XLA Modules:
  0.0 225.8 jit_solution(8974080776366906724)
XLA Ops:
  0.6 212.2 %shard_map.58 = (f32[2,512,2048]{2,1,0:T(8,128)S(1)}, f32[2,512,2048]{2,1,0:T(8,128)S(1)}, bf16[2,256,16384]{2,1,0:T(8,128)(2,1)S(1)}) custom-call(bf16[2,256,16384]{2,1,0:T(8,128)(2,1)} %bitcast.1, f32[2,512,2048]{2,1,0:T(8,128)} %master.1, f32[2,512,2048]{2,1,0:T(8,128)} %momentum.1), custom_call_target="tpu_custom_call" | custom-call | tf_op jit(solution)/shard_map/pallas_call | solution.py:252
  212.9 3.4 %copy.9 = f32[2,512,2048]{2,1,0:T(8,128)} copy(f32[2,512,2048]{2,1,0:T(8,128)S(1)} %get-tuple-element.3) | data formatting | bytes 16777216
  216.3 3.4 %copy.10 = f32[2,512,2048]{2,1,0:T(8,128)} copy(f32[2,512,2048]{2,1,0:T(8,128)S(1)} %get-tuple-element.4) | data formatting | bytes 16777216
  219.7 6.2 %copy.11 = bf16[2,256,16384]{2,1,0:T(8,128)(2,1)} copy(bf16[2,256,16384]{2,1,0:T(8,128)(2,1)S(1)} %get-tuple-element.5) | data formatting | bytes 33554432

commit v2 on v1

--- a/solution.py
+++ b/solution.py
@@ -10,12 +10,13 @@
 F32, BF16 = jnp.float32, jnp.bfloat16
 SPLITS = 16
 AHEAD = 8
-LAGS = (4, 8, 12, 15)
+PIECES = 4
+LAGS = (6, 10, 14, 18)
 
 
 def kernel(
     dims, delta, master, momentum, mas, mom, out,
-    half, cross, total,
+    half, cross, total, first,
     load, load_own, sent, pair_in, cross_in, total_in, back_in, side_in, last_in,
 ):
     R, F, PROJ, RB, FF, WD, H = dims
@@ -52,6 +53,8 @@
         r = pl.ds(pl.multiple_of(h * S, S), S)
         return pltpu.make_async_copy(delta.at[core, r], out.at[core, r], load_own.at[h])
 
+    load_first = pltpu.make_async_copy(delta.at[other, pl.ds(0, S)], first, load.at[2])
+    load_first.start()
     barrier = pltpu.get_barrier_semaphore()
 
     def greet(device):
@@ -94,7 +97,15 @@
 
     def send_pair(t):
         c = cols(block(other, t))
-        to(delta.at[other, rows(t), c], half.at[rows(t), c], sent.at[0], pair_in.at[t], pair).start()
+        dst, sem = half.at[rows(t), c], pair_in.at[t]
+
+        @pl.when(t < F)
+        def _():
+            to(first.at[:, c], dst, sent.at[0], sem, pair).start()
+
+        @pl.when(t >= F)
+        def _():
+            to(delta.at[other, rows(t), c], dst, sent.at[0], sem, pair).start()
 
     def step_cross(t):
         @pl.when(lax.rem(t, F) == 0)
@@ -175,6 +186,8 @@
         pltpu.make_async_copy(tile, tile, side_in.at[t]).wait()
         to(tile, tile, sent.at[5], last_in, pair).start()
 
+    load_first.wait()
+
     @pl.loop(0, min(AHEAD, T))
     def _(t):
         send_pair(t)
@@ -237,6 +250,21 @@
     def _():
         drain_blocks(F, sent.at[2])
         drain_blocks(PROJ * B, sent.at[3])
+
+
+def store(*refs):
+    sources, targets, sem = refs[:3], refs[3:6], refs[6]
+    copies = []
+    for j, (src, dst) in enumerate(zip(sources, targets)):
+        rows = src.shape[1] // PIECES
+        for i in range(src.shape[0]):
+            for k in range(PIECES):
+                r = pl.ds(k * rows, rows)
+                copies.append(pltpu.make_async_copy(src.at[i, r], dst.at[i, r], sem.at[j, i, k]))
+    for copy in copies:
+        copy.start()
+    for copy in copies:
+        copy.wait()
 
 
 def on_device(deltas, master, momentum):
@@ -262,14 +290,22 @@
             pltpu.VMEM((RB, FF), BF16),
             pltpu.VMEM((RB, FF), BF16),
             pltpu.VMEM(master.shape, BF16),
-            dma((2,)), dma((H,)), dma((6,)),
+            pltpu.VMEM((RB // H, FF), BF16),
+            dma((3,)), dma((H,)), dma((6,)),
             dma((T,)), dma((T,)), dma((PROJ * B * H,)), dma((T,)), dma((T,)), dma,
         ],
         compiler_params=pltpu.CompilerParams(
             collective_id=0, has_side_effects=True, vmem_limit_bytes=24 * 2**20
         ),
     )(local, master, momentum)
-    return results
+    return pl.pallas_call(
+        store,
+        out_shape=[jax.ShapeDtypeStruct(r.shape, r.dtype) for r in results],
+        in_specs=[vmem] * 3,
+        out_specs=[hbm] * 3,
+        scratch_shapes=[dma((3, PROJ, PIECES))],
+        compiler_params=pltpu.CompilerParams(vmem_limit_bytes=2**20),
+    )(*(pltpu.with_memory_space_constraint(r, pltpu.VMEM) for r in results))
 
 
 def solution(mesh):

time: 226 us -> 223 us (0.987)
  local copies, waits for them, and re-layouts: 13 us -> 0 us
  Pallas kernels: 212 us -> 222 us
    unnamed x3 -> x0, local copies, waits for them, and re-layouts: 13 us -> none
    pallas_call x0 -> x1, Pallas kernels: none -> 11.1 us  [on_device(): pl.pallas_call(store, out_shape=[jax.ShapeDtypeStruct(r.shape, r.dtype) f...]
where the time goes in v2:
time: 223 us
  Pallas kernels  222 us (100%)
    pallas_call x1, Pallas kernels, on_device(): pl.pallas_call(functools.partial(kernel, (R, F, PROJ, RB, FF, WD, H)), ou...  211 us
    pallas_call x1, Pallas kernels, on_device(): pl.pallas_call(store, out_shape=[jax.ShapeDtypeStruct(r.shape, r.dtype) f...  11.1 us

profile of v2, /device:TPU:3, one launch (start us, length us, event | category | flops | bytes accessed | tf_op | source)
XLA Modules:
  0.0 222.7 jit_solution(5758118453603235730)
XLA Ops:
  0.6 210.9 %shard_map.58 = (f32[2,512,2048]{2,1,0:T(8,128)S(1)}, f32[2,512,2048]{2,1,0:T(8,128)S(1)}, bf16[2,256,16384]{2,1,0:T(8,128)(2,1)S(1)}) custom-call(bf16[2,256,16384]{2,1,0:T(8,128)(2,1)} %bitcast.1, f32[2,512,2048]{2,1,0:T(8,128)} %master.1, f32[2,512,2048]{2,1,0:T(8,128)} %momentum.1), custom_call_target="tpu_custom_call" | custom-call | tf_op jit(solution)/shard_map/pallas_call | solution.py:280
  211.5 11.1 %shard_map.59 = (f32[2,512,2048]{2,1,0:T(8,128)}, f32[2,512,2048]{2,1,0:T(8,128)}, bf16[2,256,16384]{2,1,0:T(8,128)(2,1)}) custom-call(f32[2,512,2048]{2,1,0:T(8,128)S(1)} %get-tuple-element.6.refs_0_, f32[2,512,2048]{2,1,0:T(8,128)S(1)} %get-tuple-element.7.refs_1_, bf16[2,256,16384]{2,1,0:T(8,128)(2,1)S(1)} %get-tuple-element.8.refs_2_), custom_call_target="tpu_custom_call" | custom-call | tf_op jit(solution)/shard_map/pallas_call | solution.py:301

commit v3 on v2

--- a/solution.py
+++ b/solution.py
@@ -11,6 +11,7 @@
 SPLITS = 16
 AHEAD = 8
 PIECES = 4
+CATCH = 3
 LAGS = (6, 10, 14, 18)
 
 
@@ -215,6 +216,8 @@
             load_mas.wait()
             load_mom.wait()
 
+        catch = min(CATCH, T // 2)
+
         def late(lag, on, step):
             @pl.when(jnp.logical_and(on, jnp.logical_and(t >= lag, t < T + lag)))
             def _():
@@ -222,7 +225,9 @@
 
         late(LAGS[0], near, step_total)
         late(LAGS[1], True, step_update)
-        late(LAGS[2], near, step_side)
+        begun = t - (T + LAGS[0] - catch)
+        late(LAGS[2] - jnp.clip(begun, 0, catch), near, step_side)
+        late(LAGS[2] - jnp.clip(begun, 0, catch) - 1, jnp.logical_and(near, jnp.logical_and(begun >= 0, begun < catch)), step_side)
         late(LAGS[3], far, step_pair)
 
     drain(out.at[other], last_in)

time: 223 us -> 223 us (level)
  no operation moved by 1% of the time
where the time goes in v3:
time: 223 us
  Pallas kernels  222 us (100%)
    pallas_call x1, Pallas kernels, on_device(): pl.pallas_call(functools.partial(kernel, (R, F, PROJ, RB, FF, WD, H)), ou...  211 us
    pallas_call x1, Pallas kernels, on_device(): pl.pallas_call(store, out_shape=[jax.ShapeDtypeStruct(r.shape, r.dtype) f...  11.1 us

profile of v3, /device:TPU:3, one launch (start us, length us, event | category | flops | bytes accessed | tf_op | source)
XLA Modules:
  0.0 222.7 jit_solution(16605422515781752500)
XLA Ops:
  0.6 211.0 %shard_map.58 = (f32[2,512,2048]{2,1,0:T(8,128)S(1)}, f32[2,512,2048]{2,1,0:T(8,128)S(1)}, bf16[2,256,16384]{2,1,0:T(8,128)(2,1)S(1)}) custom-call(bf16[2,256,16384]{2,1,0:T(8,128)(2,1)} %bitcast.1, f32[2,512,2048]{2,1,0:T(8,128)} %master.1, f32[2,512,2048]{2,1,0:T(8,128)} %momentum.1), custom_call_target="tpu_custom_call" | custom-call | tf_op jit(solution)/shard_map/pallas_call | solution.py:285
  211.6 11.1 %shard_map.59 = (f32[2,512,2048]{2,1,0:T(8,128)}, f32[2,512,2048]{2,1,0:T(8,128)}, bf16[2,256,16384]{2,1,0:T(8,128)(2,1)}) custom-call(f32[2,512,2048]{2,1,0:T(8,128)S(1)} %get-tuple-element.6.refs_0_, f32[2,512,2048]{2,1,0:T(8,128)S(1)} %get-tuple-element.7.refs_1_, bf16[2,256,16384]{2,1,0:T(8,128)(2,1)S(1)} %get-tuple-element.8.refs_2_), custom_call_target="tpu_custom_call" | custom-call | tf_op jit(solution)/shard_map/pallas_call | solution.py:306
